TPU v7x, 32 devices: a whole 2x2x4 slice. The times are simulated.
32 devices in a mesh: chan: 8 (over z, x), slab: 4 (over y, core).
Axes of the slice: x: 2, y: 2, z: 4, core: 2. Of those that a mesh axis runs over, the one named last changes fastest.
Arguments:
- volume_now: float32 [64, 4, 16, 512], P('chan', 'slab'), may hold values from 0.05 to 22
- extrapolated: float32 [64, 4, 16, 512], P('chan', 'slab'), may hold values from -5 to 24
- dual_grad: float32 [3, 64, 4, 16, 512], P(None, 'chan', 'slab'), may hold values from -3 to 3
- dual_data: float32 [64, 4, 4096], P('chan', 'slab'), may hold values from -6 to 6
- measured: float32 [64, 4, 4096], P('chan', 'slab'), may hold values from -6 to 18
- projector: bfloat16 [64, 128, 128], replicated, may hold values from -0.375 to 0.375
- tile_rows: int32 [64], replicated, may hold values from 0 to 31
- tile_cols: int32 [64], replicated, may hold values from 0 to 63
- dual_step: float32 [1], replicated, may hold values from 0.3 to 0.6
- primal_step: float32 [1], replicated, may hold values from 0.2 to 0.5
- reg_weight: float32 [1], replicated, may hold values from 1.2 to 2.4
Outputs:
- updated: float32 [64, 4, 16, 512], P('chan', 'slab')
- dual_grad_new: float32 [3, 64, 4, 16, 512], P(None, 'chan', 'slab')
- dual_data_new: float32 [64, 4, 4096], P('chan', 'slab')
- totals: float32 [2], replicated
Inputs may be any that keep to these rules, and one draw needn't show every extreme that they name: `tile_rows`: ray block of each tile; several tiles may share a block. `tile_cols`: pixel block of each tile, blocks counted along the row-by-row pixel order.
All inputs are finite; a program needn't handle non-finite values.
Results may differ from a plain program's by a relative error of at most 0.002.
Values sent between devices are 32-bit elements; how exact they have to be, the bound alone decides.
A program may use at most 64 MiB of HBM per device.

v0:
```python
import math

import jax
import jax.numpy as jnp
from jax import lax
from jax.sharding import PartitionSpec as P

SWEEPS = 6


index_pairs = ((0, 0), (1, 1), (2, 2), (0, 1), (0, 2), (1, 2))
sweep_order = ((0, 1), (0, 2), (1, 2))


def from_behind(block, axis, distance):
    devices = range(lax.axis_size(axis))
    route = [(i - distance, i) for i in devices if i - distance in devices]
    return lax.ppermute(block, axis, route)


def rotate_columns(matrix, first_idx, second_idx, cosine, sine_value):
    result = [list(row) for row in matrix]
    for row_idx in range(3):
        left_val = matrix[row_idx][first_idx]
        right_val = matrix[row_idx][second_idx]
        result[row_idx][first_idx] = cosine * left_val - sine_value * right_val
        result[row_idx][second_idx] = sine_value * left_val + cosine * right_val
    return result


def rotate_rows(matrix, first_idx, second_idx, cosine, sine_value):
    result = [list(row) for row in matrix]
    for col_idx in range(3):
        upper_val = matrix[first_idx][col_idx]
        lower_val = matrix[second_idx][col_idx]
        result[first_idx][col_idx] = cosine * upper_val - sine_value * lower_val
        result[second_idx][col_idx] = sine_value * upper_val + cosine * lower_val
    return result


def unpack(entry_list):
    return [
        [entry_list[0], entry_list[3], entry_list[4]],
        [entry_list[3], entry_list[1], entry_list[5]],
        [entry_list[4], entry_list[5], entry_list[2]],
    ]


def pack_entries(matrix):
    return jnp.stack([matrix[first_idx][second_idx] for first_idx, second_idx in index_pairs])


def spectral_factor(matrix, radius):
    vectors = [[1.0 if row_idx == col_idx else 0.0 for col_idx in range(3)] for row_idx in range(3)]
    for sweep_idx in range(SWEEPS):
        for first_idx, second_idx in sweep_order:
            angle_half = 0.5 * jnp.arctan2(
                2.0 * matrix[first_idx][second_idx],
                matrix[second_idx][second_idx] - matrix[first_idx][first_idx],
            )
            cosine = jnp.cos(angle_half)
            sine_value = jnp.sin(angle_half)
            matrix = rotate_rows(
                rotate_columns(matrix, first_idx, second_idx, cosine, sine_value),
                first_idx,
                second_idx,
                cosine,
                sine_value,
            )
            vectors = rotate_columns(vectors, first_idx, second_idx, cosine, sine_value)
    root_values = [jnp.sqrt(jnp.maximum(matrix[diag_idx][diag_idx], 0.0)) for diag_idx in range(3)]
    scales = [radius / jnp.maximum(root_values[diag_idx], radius) for diag_idx in range(3)]
    factor = [
        [
            vectors[row_idx][0] * scales[0] * vectors[col_idx][0]
            + vectors[row_idx][1] * scales[1] * vectors[col_idx][1]
            + vectors[row_idx][2] * scales[2] * vectors[col_idx][2]
            for col_idx in range(3)
        ]
        for row_idx in range(3)
    ]
    excess = (
        jnp.maximum(root_values[0] - radius, 0.0)
        + jnp.maximum(root_values[1] - radius, 0.0)
        + jnp.maximum(root_values[2] - radius, 0.0)
    ) / radius
    return (factor, excess)


def apply_factor(candidate, matrix):
    return jnp.stack(
        [
            candidate[0] * matrix[0][col_idx]
            + candidate[1] * matrix[1][col_idx]
            + candidate[2] * matrix[2][col_idx]
            for col_idx in range(3)
        ]
    )


def forward_difference(volume, along_axis):
    length = volume.shape[along_axis]
    later = lax.slice_in_dim(volume, 1, length, axis=along_axis)
    kept_part = lax.slice_in_dim(volume, 0, length - 1, axis=along_axis)
    zero_layer = jnp.zeros_like(lax.slice_in_dim(volume, 0, 1, axis=along_axis))
    return jnp.concatenate([later - kept_part, zero_layer], axis=along_axis)


def backward_difference(component, along_axis):
    length = component.shape[along_axis]
    kept_part = lax.slice_in_dim(component, 0, length - 1, axis=along_axis)
    zero_layer = jnp.zeros_like(lax.slice_in_dim(component, 0, 1, axis=along_axis))
    masked = jnp.concatenate([kept_part, zero_layer], axis=along_axis)
    earlier = jnp.concatenate([zero_layer, kept_part], axis=along_axis)
    return masked - earlier


def project_forward(rounded, projector, tile_rows, tile_cols, rays):
    channels, slices, pixels = rounded.shape
    tile_edge = projector.shape[1]
    row_blocks = rays // tile_edge
    blocks = rounded.reshape(channels * slices, pixels // tile_edge, tile_edge)
    picked = jnp.take(blocks, tile_cols, axis=1)
    products = jnp.einsum("tij,btj->bti", projector, picked, preferred_element_type=jnp.float32)
    selector = (tile_rows[:, None] == jnp.arange(row_blocks, dtype=jnp.int32)[None, :]).astype(
        jnp.float32
    )
    sinogram = jnp.einsum("tr,bti->bri", selector, products, precision=lax.Precision.HIGHEST)
    return sinogram.reshape(channels, slices, rays)


def project_back(data_low, projector, tile_rows, tile_cols, pixels):
    channels, slices, rays = data_low.shape
    tile_edge = projector.shape[1]
    col_blocks = pixels // tile_edge
    blocks = data_low.reshape(channels * slices, rays // tile_edge, tile_edge)
    picked = jnp.take(blocks, tile_rows, axis=1)
    products = jnp.einsum("tij,bti->btj", projector, picked, preferred_element_type=jnp.float32)
    selector = (tile_cols[:, None] == jnp.arange(col_blocks, dtype=jnp.int32)[None, :]).astype(
        jnp.float32
    )
    volume = jnp.einsum("tc,btj->bcj", selector, products, precision=lax.Precision.HIGHEST)
    return volume.reshape(channels, slices, pixels)


def on_device(
    volume_now,
    extrapolated,
    dual_grad,
    dual_data,
    measured,
    projector,
    tile_rows,
    tile_cols,
    dual_step,
    primal_step,
    reg_weight,
):
    dual_rate = dual_step[0]
    primal_rate = primal_step[0]
    channels, slices, row_count, col_count = volume_now.shape
    pixels = row_count * col_count
    rays = dual_data.shape[2]
    chan_count = lax.axis_size("chan")
    slab_count = lax.axis_size("slab")
    total_channels = channels * chan_count
    last_slice = lax.axis_index("slab") == slab_count - 1
    following = from_behind(extrapolated, "slab", -1)
    rounded = extrapolated.reshape(channels, slices, pixels).astype(jnp.bfloat16)
    projected = project_forward(rounded, projector, tile_rows, tile_cols, rays)
    residual = projected - measured
    data_new = (dual_data + dual_rate * residual) / (1.0 + dual_rate)
    misfit_part = jnp.sum(residual * residual)
    across = jnp.where(last_slice, 0.0, following - extrapolated)
    gradient = jnp.stack(
        [forward_difference(extrapolated, 2), forward_difference(extrapolated, 3), across]
    )
    candidate = dual_grad + dual_rate * gradient
    partial_gram = jnp.stack(
        [
            jnp.sum(candidate[first_idx] * candidate[second_idx], axis=0)
            for first_idx, second_idx in index_pairs
        ]
    ).reshape(6, slices * pixels)
    radius = reg_weight[0] * math.sqrt(total_channels)
    gram_rows = lax.psum(partial_gram, "chan")
    factor, excess = spectral_factor(
        unpack([gram_rows[entry_idx] for entry_idx in range(6)]), radius
    )
    factor_rows = pack_entries(factor)
    share_length = excess.shape[0] // chan_count
    own_share = lax.dynamic_slice_in_dim(
        excess, lax.axis_index("chan") * share_length, share_length
    )
    combined = lax.psum(jnp.stack([misfit_part, jnp.sum(own_share)]), ("chan", "slab"))
    matrix = unpack(
        [factor_rows[entry_idx].reshape(slices, row_count, col_count) for entry_idx in range(6)]
    )
    grad_new = apply_factor(candidate, matrix)
    prior_layer = from_behind(grad_new[2], "slab", 1)
    masked = jnp.where(last_slice, 0.0, grad_new[2])
    divergence = (
        backward_difference(grad_new[0], 2)
        + backward_difference(grad_new[1], 3)
        + masked
        - prior_layer
    )
    data_low = data_new.astype(jnp.bfloat16)
    back_proj = project_back(data_low, projector, tile_rows, tile_cols, pixels).reshape(
        volume_now.shape
    )
    updated = jnp.maximum(volume_now - primal_rate * (back_proj - divergence), 0.0)
    totals = jnp.stack(
        [
            combined[0] / (total_channels * slab_count * slices * rays),
            combined[1] / (slab_count * slices * pixels),
        ]
    )
    return (updated, grad_new, data_new, totals)


def solution(mesh):
    placed = (
        P("chan", "slab", None, None),
        P("chan", "slab", None, None),
        P(None, "chan", "slab", None, None),
        P("chan", "slab", None),
        P("chan", "slab", None),
        P(),
        P(),
        P(),
        P(),
        P(),
        P(),
    )
    return jax.shard_map(
        on_device,
        mesh=mesh,
        in_specs=placed,
        out_specs=(
            P("chan", "slab", None, None),
            P(None, "chan", "slab", None, None),
            P("chan", "slab", None),
            P(),
        ),
        check_vma=False,
    )
```

profile of v0, /device:TPU:1, one launch (start us, length us, event | category | flops | bytes accessed | tf_op | source)
XLA Modules:
  0.0 178.3 jit_solution(11393200533945876407)
XLA Ops:
  7.2 2.1 %collective-permute-start = (f32[8,1,16,512]{3,2,0,1:T(8,128)}, f32[8,1,16,512]{3,2,0,1:T(8,128)}, u32[]{:S(2)}, u32[]{:S(2)}) collective-permute-start(f32[8,1,16,512]{3,2,0,1:T(8,128)} %bitcast.145), channel_id=1, source_target_pairs={{1,0},{2,1},{3,2},{5,4},{6,5},{7,6},{9,8},{10,9},{11,10},{13,12},{... | collective-permute-start | bytes 786440 | tf_op jit(solution)/shard_map/ppermute | solution.py:18
  9.3 1.2 slice_subtract_fusion
  10.5 1.1 slice_subtract_fusion.1
  11.6 1.0 convert_element_type.14
  12.5 0.7 compare_select_fusion
  13.2 0.7 compare_and_fusion
  13.9 0.7 compare_select_fusion.1
  14.5 0.7 compare_and_fusion.1
  16.0 0.6 gather_fusion
  16.7 1.2 convolution_bitcast_fusion.2
  18.2 1.9 %convert_reduce_fusion = (bf16[8,4096]{1,0:T(8,128)(2,1)S(1)}, f32[8,1,4096]{2,1,0:T(1,128)}) fusion(f32[]{:T(128)S(6)} %add.3420, f32[8,1,4096]{2,1,0:T(1,128)} %param.14, f32[8,1,4096]{2,1,0:T(1,128)S(1)} %bitcast.150, f32[8,1,4096]{2,1,0:T(1,128)} %param.15, f32[]{:T(128)} %bitcast.141), kind=kLoop, calls=%fused_computation.55 | loop fusion | flops 163840 | bytes 589832 | tf_op jit(solution)/shard_map/convert_element_type | solution.py:208
  20.2 0.6 gather_fusion.1
  20.8 1.4 convolution_bitcast_fusion.1
  22.2 1.0 select_bitcast_fusion
  23.8 1.0 stack.63
  25.8 0.7 reshape_reshape.3
  27.2 1.9 %multiply_reduce_fusion = f32[]{:T(128)} fusion(f32[8,1,4096]{2,1,0:T(1,128)S(1)} %bitcast.151, f32[8,1,4096]{2,1,0:T(1,128)} %param.15), kind=kLoop, calls=%fused_computation.54 | loop fusion | flops 98303 | bytes 262148 | tf_op jit(solution)/shard_map/reduce_sum | solution.py:173
  29.0 68.0 %all-reduce.6.cloned.1.call-done = f32[6,8192]{1,0:T(8,128)} async-done(((f32[6,8192]{1,0:T(8,128)}), f32[6,8192]{1,0:T(8,128)}) %all-reduce.6.cloned.1.call-update) | async-done | bytes 196624 | tf_op jit(solution)/shard_map/psum | solution.py:186
  97.0 2.4 %slice_reduce_fusion.2 = (f32[8192]{0:T(1024)S(1)}, f32[8192]{0:T(1024)S(1)}, f32[8192]{0:T(1024)S(1)}, f32[8192]{0:T(1024)S(1)}, f32[8192]{0:T(1024)S(1)}, /*in...) fusion(f32[6,8192]{1,0:T(8,128)} %all-reduce.6.cloned.1.call-done), kind=kLoop, calls=%fused_computation.703 | loop fusion | bytes 589824 | tf_op jit(solution)/shard_map/slice | solution.py:188
  99.5 0.9 multiply_add_fusion.83
  100.4 0.6 multiply_add_fusion.82
  101.0 1.0 multiply_add_fusion.61
  102.0 0.6 multiply_add_fusion.60
  102.6 0.4 multiply_subtract_fusion.68
  103.0 0.9 multiply_add_fusion.52
  103.9 0.4 multiply_subtract_fusion.43
  104.3 0.8 multiply_subtract_fusion.22
  105.1 0.6 multiply_add_fusion.30
  105.7 0.4 multiply_subtract_fusion.34
  106.3 1.0 multiply_subtract_fusion.16
  107.4 0.4 multiply_subtract_fusion.4
  108.0 0.9 subtract_maximum_fusion.1
  108.9 0.7 subtract_maximum_fusion
  109.8 0.6 fusion.45
  110.4 1.4 pad_maximum_fusion.1
  112.0 0.7 multiply_subtract_fusion.143
  112.9 0.7 multiply_subtract_fusion.140
  113.8 0.7 multiply_subtract_fusion.137
  114.7 0.7 multiply_subtract_fusion.134
  115.6 0.7 multiply_add_fusion.141
  117.3 1.0 multiply_add_fusion.2
  118.3 0.8 fusion.5
  119.1 40.5 %psum.15 = f32[2]{0:T(128)S(1)} all-reduce(f32[2]{0:T(128)S(1)} %pad_maximum_fusion.1), channel_id=1, replica_groups=mesh['chan'=8,'slab'=4] {'chan','slab'}, use_global_device_ids=true, to_apply=%region_9.10 | all-reduce | flops 2 | bytes 16 | tf_op jit(solution)/shard_map/psum | solution.py:195
  159.6 5.3 %collective-permute-start.1 = (f32[8,1,16,512]{3,2,0,1:T(8,128)}, f32[8,1,16,512]{3,2,0,1:T(8,128)S(1)}, u32[]{:S(2)}, u32[]{:S(2)}) collective-permute-start(f32[8,1,16,512]{3,2,0,1:T(8,128)} %get-tuple-element.385), channel_id=1, source_target_pairs={{0,1},{1,2},{2,3},{4,5},{5,6},{6,7},{8,9},{9,10},{10,11},{12,13},{... | collective-permute-start | bytes 786440 | tf_op jit(solution)/shard_map/ppermute | solution.py:18
  164.9 0.6 fusion.156
  166.8 0.6 pad_maximum_fusion.2
  167.3 2.1 %pad_maximum_fusion = f32[3,8,1,16,512]{4,3,2,1,0:T(8,128)} fusion(f32[1,8,1,16,512]{4,3,2,1,0:T(8,128)} %get-tuple-element.382, f32[1,8,1,16,512]{4,3,2,1,0:T(8,128)} %get-tuple-element.381, f32[1,8,1,16,512]{4,3,2,1,0:T(8,128)} %get-tuple-element.380), kind=kLoop, calls=%fused_computation.8 | loop fusion | flops 393216 | bytes 1572864 | tf_op jit(solution)/shard_map/stack | solution.py:91
  169.4 2.0 %fusion.15 = f32[8,1,16,512]{3,2,1,0:T(8,128)} fusion(f32[8,1,16,512]{3,2,1,0:T(8,128)} %param.11, f32[8,1,16,512]{3,2,0,1:T(8,128)} %reshape_reshape.3, f32[8,1,16,512]{3,2,0,1:T(8,128)S(1)} %collective-permute-done.1, f32[8,1,16,512]{3,2,0,1:T(8,128)} %get-tuple-element.385, f32[8,1,16,511]{3,2,0,1:T(8,128)S(1)} %bitcast.149, ...), kind=kLoop, calls=%fused_computation.40 | loop fusion | flops 786432 | bytes 2342933
  (63 shorter events, 3.8 us)
Async XLA Ops:
  7.2 9.5 %copy-start = (bf16[64,128,128]{2,1,0:T(8,128)(2,1)S(1)}, bf16[64,128,128]{2,1,0:T(8,128)(2,1)}, u32[]{:S(2)}) copy-start(bf16[64,128,128]{2,1,0:T(8,128)(2,1)} %param.16) | copy-start | bytes 6291460
  7.2 89.9 %all-reduce.6.cloned.1.call-start = ((), (), s32[]{:S(2)}) async-start(), calls=%async_computation | async-start | bytes 524288 | tf_op jit(solution)/shard_map/psum | solution.py:186
  7.2 15.0 %collective-permute-start = (f32[8,1,16,512]{3,2,0,1:T(8,128)}, f32[8,1,16,512]{3,2,0,1:T(8,128)}, u32[]{:S(2)}, u32[]{:S(2)}) collective-permute-start(f32[8,1,16,512]{3,2,0,1:T(8,128)} %bitcast.145), channel_id=1, source_target_pairs={{1,0},{2,1},{3,2},{5,4},{6,5},{7,6},{9,8},{10,9},{11,10},{13,12},{... | collective-permute-start | bytes 786440 | tf_op jit(solution)/shard_map/ppermute | solution.py:18
  10.5 7.4 %copy-start.4 = (s32[64]{0:T(128)S(1)}, s32[64]{0:T(128)}, u32[]{:S(2)}) copy-start(s32[64]{0:T(128)} %param.17) | copy-start | bytes 772
  18.2 4.1 %copy-start.1 = (f32[8,1,16,512]{3,2,1,0:T(8,128)S(1)}, f32[8,1,16,512]{3,2,1,0:T(8,128)}, u32[]{:S(2)}) copy-start(f32[8,1,16,512]{3,2,1,0:T(8,128)} %param.12) | copy-start | bytes 786436
  20.8 2.4 %copy-start.3 = (f32[3,8,1,16,512]{4,3,2,1,0:T(8,128)S(1)}, f32[3,8,1,16,512]{4,3,2,1,0:T(8,128)}, u32[]{:S(2)}) copy-start(f32[3,8,1,16,512]{4,3,2,1,0:T(8,128)} %param.13) | copy-start | bytes 2359300
  23.2 1.6 copy-start.5
  23.4 1.4 copy-start.2
  118.3 51.2 %copy-start.6 = (pred[16]{0:T(512)(128)(4,1)S(1)}, pred[16]{0:T(512)(128)(4,1)}, u32[]{:S(2)}) copy-start(pred[16]{0:T(512)(128)(4,1)} %constant.35.clone.1) | copy-start | bytes 52
  118.3 51.2 %copy-start.7 = (pred[512]{0:T(512)(128)(4,1)S(1)}, pred[512]{0:T(512)(128)(4,1)}, u32[]{:S(2)}) copy-start(pred[512]{0:T(512)(128)(4,1)} %constant.66.clone.1) | copy-start | bytes 1540
  159.6 9.8 %collective-permute-start.1 = (f32[8,1,16,512]{3,2,0,1:T(8,128)}, f32[8,1,16,512]{3,2,0,1:T(8,128)S(1)}, u32[]{:S(2)}, u32[]{:S(2)}) collective-permute-start(f32[8,1,16,512]{3,2,0,1:T(8,128)} %get-tuple-element.385), channel_id=1, source_target_pairs={{0,1},{1,2},{2,3},{4,5},{5,6},{6,7},{8,9},{9,10},{10,11},{12,13},{... | collective-permute-start | bytes 786440 | tf_op jit(solution)/shard_map/ppermute | solution.py:18
Sparse Core Ops, SparseCore 0:
  24.9 72.0 all-reduce.5
where the time goes:
time: 179 us; the launch traced here: 178 us
  waiting for transfers between devices  68 us (38%)
  blocking collectives  40.5 us (23%)
  other arithmetic  34.9 us (19%)
  between operations  17.8 us (10%)
  starting transfers between devices  7.35 us (4%)
  local copies, waits for them, and re-layouts  6.49 us (4%)
  matrix products  3.18 us (2%)
    psum x1, waiting for transfers between devices, on_device(): gram_rows = lax.psum(partial_gram, 'chan')  68 us
    psum x1, blocking collectives, on_device(): lax.psum(jnp.stack([misfit_part, jnp.sum(own_share)]), ('chan', 'slab'))  40.5 us
    ppermute x2, starting transfers between devices, from_behind(): return lax.ppermute(block, axis, route)  7.32 us
    sub x11, other arithmetic, rotate_columns(): result[row_idx][first_idx] = cosine * left_val - sine_value * right_val  4.83 us
    add x8, other arithmetic, rotate_rows(): result[second_idx][col_idx] = sine_value * upper_val + cosine * lower_val  4.13 us
  transfers between devices with their start and end apart: 3, of which 1 were waited for; matrix products, arithmetic and copies ran while one was open for 10% of the time, Pallas kernels for 0%

commit v1 on v0

v1 whole, which is shorter than its diff:
```python
import functools
import math

import jax
import jax.numpy as jnp
from jax import lax
from jax.experimental import pallas as pl
from jax.experimental.pallas import tpu as pltpu
from jax.sharding import PartitionSpec as P

SWEEPS = 6
LANES = 128
SUBS = 8

index_pairs = ((0, 0), (1, 1), (2, 2), (0, 1), (0, 2), (1, 2))
sweep_order = ((0, 1, 2), (0, 2, 1), (1, 2, 0))
entry_of = {pair: idx for idx, pair in enumerate(index_pairs)}
entry_of.update({(b, a): idx for (a, b), idx in list(entry_of.items())})


def each(start, stop, body):
    if stop - start <= 16:
        for i in range(start, stop):
            body(i)
    else:

        def step(i, carry):
            body(i)
            return carry

        lax.fori_loop(start, stop, step, 0)


def tomography(
    rows_ref, cols_ref, rate_ref, ext_ref, dual_ref, meas_ref, proj_ref,
    data_ref, back_ref, misfit_ref, image, sino, low, back,
):
    channels, row_count, col_count = ext_ref.shape
    per_row = col_count // LANES
    ray_blocks = sino.shape[0]
    tiles = proj_ref.shape[0]
    together = math.gcd(tiles, 8)
    rate = rate_ref[0]
    for row in range(row_count):
        line = ext_ref[:, row, :].astype(jnp.bfloat16).astype(jnp.float32)
        for q in range(per_row):
            image[row * per_row + q] = line[:, q * LANES : (q + 1) * LANES]
    sino[...] = jnp.zeros_like(sino)
    back[...] = jnp.zeros_like(back)

    def forward(step, carry):
        base = step * together
        made = []
        for u in range(together):
            picked = image[cols_ref[base + u]].astype(jnp.bfloat16)
            made.append(
                lax.dot_general(
                    picked, proj_ref[base + u], (((1,), (1,)), ((), ())),
                    preferred_element_type=jnp.float32,
                )
            )
        for u in range(together):
            spot = rows_ref[base + u]
            sino[spot] = sino[spot] + made[u]
        return carry

    lax.fori_loop(0, tiles // together, forward, 0)

    inverse = 1.0 / (1.0 + jnp.full((channels, LANES), rate, jnp.float32))
    misfit = jnp.zeros((channels, LANES), jnp.float32)
    for r in range(ray_blocks):
        residual = sino[r] - meas_ref[:, r, :]
        fresh = (dual_ref[:, r, :] + rate * residual) * inverse
        misfit = misfit + residual * residual
        data_ref[:, r, :] = fresh
        low[r] = fresh
    misfit_ref[...] = misfit

    def backward(step, carry):
        base = step * together
        made = []
        for u in range(together):
            picked = low[rows_ref[base + u]].astype(jnp.bfloat16)
            made.append(
                lax.dot_general(
                    picked, proj_ref[base + u], (((1,), (0,)), ((), ())),
                    preferred_element_type=jnp.float32,
                )
            )
        for u in range(together):
            spot = cols_ref[base + u]
            back[spot] = back[spot] + made[u]
        return carry

    lax.fori_loop(0, tiles // together, backward, 0)
    for row in range(row_count):
        back_ref[:, row, :] = jnp.concatenate(
            [back[row * per_row + q] for q in range(per_row)], axis=1
        )


def jacobi_sweep(_, state):
    sym = list(state[:6])
    vec = [list(state[6 + 3 * i : 9 + 3 * i]) for i in range(3)]
    for p, q, k in sweep_order:
        app, aqq, apq = sym[p], sym[q], sym[entry_of[(p, q)]]
        akp, akq = sym[entry_of[(k, p)]], sym[entry_of[(k, q)]]
        diff = aqq - app
        off = apq + apq
        square = diff * diff + off * off
        live = square > 1e-36
        inv = lax.rsqrt(jnp.where(live, square, 1.0))
        half = 0.5 + 0.5 * jnp.where(live, jnp.abs(diff) * inv, 1.0)
        inv_big = lax.rsqrt(half)
        big = half * inv_big
        small = jnp.where(live, 0.5 * jnp.abs(off) * inv * inv_big, 0.0)
        ahead = diff >= 0.0
        c = jnp.where(ahead, big, small)
        s_abs = jnp.where(ahead, small, big)
        s = jnp.where(off >= 0.0, s_abs, -s_abs)
        cc, ss, cross = c * c, s * s, c * s * off
        sym[p] = cc * app - cross + ss * aqq
        sym[q] = ss * app + cross + cc * aqq
        sym[entry_of[(p, q)]] = jnp.where(live, 0.0, apq)
        sym[entry_of[(k, p)]] = c * akp - s * akq
        sym[entry_of[(k, q)]] = s * akp + c * akq
        for row in range(3):
            left, right = vec[row][p], vec[row][q]
            vec[row][p] = c * left - s * right
            vec[row][q] = s * left + c * right
    return tuple(sym) + tuple(vec[0]) + tuple(vec[1]) + tuple(vec[2])


def spectral(gram, radius):
    one, zero = jnp.ones_like(gram[0]), jnp.zeros_like(gram[0])
    start = tuple(gram) + tuple(one if i % 4 == 0 else zero for i in range(9))
    state = lax.fori_loop(0, SWEEPS, jacobi_sweep, start)
    vec = [state[6 + 3 * i : 9 + 3 * i] for i in range(3)]
    radius = jnp.full(gram[0].shape, radius, jnp.float32)
    roots = [jnp.sqrt(jnp.maximum(state[i], 0.0)) for i in range(3)]
    scales = [radius / jnp.maximum(roots[i], radius) for i in range(3)]
    factor = [sum(vec[a][i] * scales[i] * vec[b][i] for i in range(3)) for a, b in index_pairs]
    excess = sum(jnp.maximum(roots[i] - radius, 0.0) for i in range(3)) / radius
    return factor, excess


def variation(
    n, slabs, owners, total_channels,
    rate_ref, primal_ref, reg_ref, vol_ref, ext_ref, grad_ref, misfit_ref, back_ref,
    upd_ref, out_ref, totals_ref,
    foll, prior, cand, level, part, gathered, fac, fac_image, sums,
    foll_send, foll_recv, prior_send, prior_recv,
    part_send, part_recv, fac_send, fac_recv, sum_send, sum_recv,
):
    channels, row_count, col_count = ext_ref.shape
    per_row = col_count // LANES
    blocks = part.shape[0]
    own = blocks // owners
    me = lax.axis_index("chan")
    slab = lax.axis_index("slab")
    last = slab == slabs - 1
    first = slab == 0
    rate = rate_ref[0]
    primal = primal_ref[0]
    radius = reg_ref[0] * math.sqrt(total_channels)

    barrier = pltpu.get_barrier_semaphore()

    def greet_chan(i):
        pl.semaphore_signal(barrier, inc=1, device_id={"chan": lax.rem(me + i, n)},
                            device_id_type=pl.DeviceIdType.MESH)

    def greet_slab(i):
        pl.semaphore_signal(barrier, inc=1, device_id={"slab": lax.rem(slab + i, slabs)},
                            device_id_type=pl.DeviceIdType.MESH)

    each(1, n, greet_chan)
    each(1, slabs, greet_slab)
    pl.semaphore_wait(barrier, n - 1 + slabs - 1)

    def foll_copy(c):
        return pltpu.make_async_remote_copy(
            src_ref=ext_ref.at[c], dst_ref=foll.at[c],
            send_sem=foll_send.at[c], recv_sem=foll_recv.at[c],
            device_id={"slab": lax.rem(slab + slabs - 1, slabs)},
            device_id_type=pl.DeviceIdType.MESH)

    def prior_copy(c):
        return pltpu.make_async_remote_copy(
            src_ref=level.at[c], dst_ref=prior.at[c],
            send_sem=prior_send.at[c], recv_sem=prior_recv.at[c],
            device_id={"slab": lax.rem(slab + 1, slabs)},
            device_id_type=pl.DeviceIdType.MESH)

    @pl.when(jnp.logical_not(first))
    def _():
        each(0, channels, lambda c: foll_copy(c).start())

    @pl.when(last)
    def _():
        foll[...] = ext_ref[...]

    @pl.when(first)
    def _():
        prior[...] = jnp.zeros_like(prior)

    row_at = lax.broadcasted_iota(jnp.int32, (row_count, col_count), 0)
    col_at = lax.broadcasted_iota(jnp.int32, (row_count, col_count), 1)

    def flat(c, carry):
        image = ext_ref[c]
        below = pltpu.roll(image, row_count - 1, 0)
        beside = pltpu.roll(image, col_count - 1, 1)
        c0 = grad_ref[0, c] + rate * jnp.where(row_at < row_count - 1, below - image, 0.0)
        c1 = grad_ref[1, c] + rate * jnp.where(col_at < col_count - 1, beside - image, 0.0)
        cand[0, c] = c0
        cand[1, c] = c1
        g0, g1, g3 = carry
        return g0 + c0 * c0, g1 + c1 * c1, g3 + c0 * c1

    def deep(c, carry):
        @pl.when(jnp.logical_not(last))
        def _():
            foll_copy(c).wait_recv()

        c2 = grad_ref[2, c] + rate * (foll[c] - ext_ref[c])
        cand[2, c] = c2
        g2, g4, g5 = carry
        return g2 + c2 * c2, g4 + cand[0, c] * c2, g5 + cand[1, c] * c2

    nothing = jnp.zeros((row_count, col_count), jnp.float32)
    g0, g1, g3 = lax.fori_loop(0, channels, flat, (nothing,) * 3)
    g2, g4, g5 = lax.fori_loop(0, channels, deep, (nothing,) * 3)
    grams = (g0, g1, g2, g3, g4, g5)

    def place(b):
        h, q = b // per_row, b % per_row
        return slice(h * SUBS, (h + 1) * SUBS), slice(q * LANES, (q + 1) * LANES)

    for b in range(blocks):
        rows, cols = place(b)
        for e in range(6):
            part[b, e] = grams[e][rows, cols]
        part[b, 6] = misfit_ref[...]

    def if_owner(index, body):
        if owners == n:
            body()
        else:
            pl.when(index < owners)(body)

    def part_copy(i):
        peer = lax.rem(me + i, n)
        return pltpu.make_async_remote_copy(
            src_ref=part.at[pl.ds(lax.rem(peer, owners) * own, own)], dst_ref=gathered.at[i],
            send_sem=part_send.at[i], recv_sem=part_recv.at[i],
            device_id={"chan": peer}, device_id_type=pl.DeviceIdType.MESH)

    def fac_copy(i):
        mine = fac.at[pl.ds(lax.rem(me, owners) * own, own)]
        return pltpu.make_async_remote_copy(
            src_ref=mine, dst_ref=mine,
            send_sem=fac_send.at[i], recv_sem=fac_recv.at[i],
            device_id={"chan": lax.rem(me + i, n)}, device_id_type=pl.DeviceIdType.MESH)

    each(1, n, lambda i: if_owner(lax.rem(me + i, n), lambda: part_copy(i).start()))

    def diagonalize():
        base = lax.rem(me, owners) * own
        gathered[0] = part[pl.ds(base, own)]
        each(1, n, lambda i: part_copy(i).wait_recv())
        if n <= 16:
            total = gathered[0]
            for i in range(1, n):
                total = total + gathered[i]
        else:
            total = lax.fori_loop(1, n, lambda i, t: t + gathered[i], gathered[0])
        factor, excess = spectral([total[:, e] for e in range(6)], radius)
        for o in range(own):
            for e in range(6):
                fac[base + o, e] = factor[e][o]
            fac[base + o, 6] = excess[o]
            fac[base + o, 7] = total[o, 6]
        each(1, n, lambda i: fac_copy(i).start())

    if_owner(me, diagonalize)
    each(1, n, lambda i: if_owner(lax.rem(me - i + n, n), lambda: fac_copy(i).wait_recv()))

    for b in range(blocks):
        rows, cols = place(b)
        for e in range(6):
            fac_image[e, rows, cols] = fac[b, e]

    def sum_copy(i):
        return pltpu.make_async_remote_copy(
            src_ref=sums.at[0], dst_ref=sums.at[i],
            send_sem=sum_send.at[i], recv_sem=sum_recv.at[i],
            device_id={"slab": lax.rem(slab + i, slabs)},
            device_id_type=pl.DeviceIdType.MESH)

    excess_sum = fac[0, 6]
    for b in range(1, blocks):
        excess_sum = excess_sum + fac[b, 6]
    sums[0, 0] = fac[0, 7]
    sums[0, 1] = excess_sum

    def turned(c, a):
        return (cand[0, c] * fac_image[entry_of[(0, a)]]
                + cand[1, c] * fac_image[entry_of[(1, a)]]
                + cand[2, c] * fac_image[entry_of[(2, a)]])

    def depth(c, carry):
        value = turned(c, 2)
        level[c] = value
        out_ref[2, c] = value

        @pl.when(jnp.logical_not(last))
        def _():
            prior_copy(c).start()

        return carry

    lax.fori_loop(0, channels, depth, 0)
    each(1, slabs, lambda i: sum_copy(i).start())
    kept = jnp.where(last, 0.0, 1.0)

    def plane(c, carry):
        n0 = turned(c, 0)
        n1 = turned(c, 1)
        out_ref[0, c] = n0
        out_ref[1, c] = n1
        q0 = jnp.where(row_at < row_count - 1, n0, 0.0)
        q1 = jnp.where(col_at < col_count - 1, n1, 0.0)
        div = (q0 - pltpu.roll(q0, 1, 0)) + (q1 - pltpu.roll(q1, 1, 1)) + kept * level[c]
        upd_ref[c] = vol_ref[c] - primal * (back_ref[c] - div)
        return carry

    lax.fori_loop(0, channels, plane, 0)

    def finish(c, carry):
        @pl.when(jnp.logical_not(first))
        def _():
            prior_copy(c).wait_recv()

        upd_ref[c] = jnp.maximum(upd_ref[c] - primal * prior[c], 0.0)
        return carry

    lax.fori_loop(0, channels, finish, 0)

    each(1, slabs, lambda i: sum_copy(i).wait_recv())
    misfit_tile, excess_tile = sums[0, 0], sums[0, 1]
    for i in range(1, slabs):
        misfit_tile = misfit_tile + sums[i, 0]
        excess_tile = excess_tile + sums[i, 1]
    totals_ref[0] = jnp.sum(misfit_tile)
    totals_ref[1] = jnp.sum(excess_tile)

    @pl.when(jnp.logical_not(first))
    def _():
        each(0, channels, lambda c: foll_copy(c).wait_send())

    @pl.when(jnp.logical_not(last))
    def _():
        each(0, channels, lambda c: prior_copy(c).wait_send())

    each(1, n, lambda i: if_owner(lax.rem(me + i, n), lambda: part_copy(i).wait_send()))
    if_owner(me, lambda: each(1, n, lambda i: fac_copy(i).wait_send()))
    each(1, slabs, lambda i: sum_copy(i).wait_send())


def on_device(
    volume_now, extrapolated, dual_grad, dual_data, measured, projector,
    tile_rows, tile_cols, dual_step, primal_step, reg_weight,
):
    channels, slices, row_count, col_count = volume_now.shape
    pixels = row_count * col_count
    rays = dual_data.shape[2]
    n = lax.axis_size("chan")
    slabs = lax.axis_size("slab")
    vmem = pl.BlockSpec(memory_space=pltpu.VMEM)
    smem = pl.BlockSpec(memory_space=pltpu.SMEM)
    f32 = jnp.float32
    image_shape = (channels, row_count, col_count)
    volume_now = volume_now.reshape(image_shape)
    extrapolated = extrapolated.reshape(image_shape)
    dual_grad = dual_grad.reshape((3,) + image_shape)
    ray_shape = (channels, rays // LANES, LANES)
    data_new, back, misfit = pl.pallas_call(
        tomography,
        out_shape=(
            jax.ShapeDtypeStruct(ray_shape, f32),
            jax.ShapeDtypeStruct(image_shape, f32),
            jax.ShapeDtypeStruct((channels, LANES), f32),
        ),
        in_specs=[smem] * 3 + [vmem] * 4,
        out_specs=(vmem,) * 3,
        scratch_shapes=[
            pltpu.VMEM((pixels // LANES, channels, LANES), f32),
            pltpu.VMEM((rays // LANES, channels, LANES), f32),
            pltpu.VMEM((rays // LANES, channels, LANES), f32),
            pltpu.VMEM((pixels // LANES, channels, LANES), f32),
        ],
        name="tomography",
    )(tile_rows, tile_cols, dual_step, extrapolated, dual_data.reshape(ray_shape),
      measured.reshape(ray_shape), projector)

    blocks = pixels // (SUBS * LANES)
    owners = math.gcd(n, blocks)
    own = blocks // owners
    dma = pltpu.SemaphoreType.DMA
    updated, grad_new, totals = pl.pallas_call(
        functools.partial(variation, n, slabs, owners, channels * n),
        out_shape=(
            jax.ShapeDtypeStruct(image_shape, f32),
            jax.ShapeDtypeStruct((3,) + image_shape, f32),
            jax.ShapeDtypeStruct((2,), f32),
        ),
        in_specs=[smem] * 3 + [vmem] * 5,
        out_specs=(vmem, vmem, smem),
        scratch_shapes=[
            pltpu.VMEM(image_shape, f32),
            pltpu.VMEM(image_shape, f32),
            pltpu.VMEM((3,) + image_shape, f32),
            pltpu.VMEM(image_shape, f32),
            pltpu.VMEM((blocks, 7, SUBS, LANES), f32),
            pltpu.VMEM((n, own, 7, SUBS, LANES), f32),
            pltpu.VMEM((blocks, 8, SUBS, LANES), f32),
            pltpu.VMEM((6, row_count, col_count), f32),
            pltpu.VMEM((slabs, 2, SUBS, LANES), f32),
            dma((channels,)), dma((channels,)), dma((channels,)), dma((channels,)),
            dma((n,)), dma((n,)), dma((n,)), dma((n,)),
            dma((slabs,)), dma((slabs,)),
        ],
        compiler_params=pltpu.CompilerParams(collective_id=0, has_side_effects=True),
        name="variation",
    )(dual_step, primal_step, reg_weight, volume_now, extrapolated, dual_grad, misfit, back)
    scale = jnp.asarray([1.0 / (channels * n * slabs * slices * rays),
                         1.0 / (slabs * slices * pixels)], f32)
    full = (channels, slices, row_count, col_count)
    return (
        updated.reshape(full),
        grad_new.reshape((3,) + full),
        data_new.reshape(channels, slices, rays),
        totals * scale,
    )


def solution(mesh):
    image = P("chan", "slab", None, None)
    duals = P(None, "chan", "slab", None, None)
    rays = P("chan", "slab", None)
    return jax.shard_map(
        on_device,
        mesh=mesh,
        in_specs=(image, image, duals, rays, rays) + (P(),) * 6,
        out_specs=(image, duals, rays, P()),
        check_vma=False,
    )
```

time: 179 us -> 43 us (0.24)
  the two profiles are of different devices: /device:TPU:1 before, /device:TPU:13 now
where the time goes in v1:
time: 43 us; the launch traced here: 42.4 us
  Pallas kernels  34.8 us (81%)
  local copies, waits for them, and re-layouts  3.76 us (9%)
  between operations  2.6 us (6%)
  other arithmetic  1.18 us (3%)
    pallas_call x1, Pallas kernels, on_device(): pl.pallas_call(functools.partial(variation, n, slabs, owners, channels *...  28.2 us
    pallas_call x1, Pallas kernels, on_device(): pl.pallas_call(tomography, out_shape=(jax.ShapeDtypeStruct(ray_shape, f32...  6.62 us
    unnamed x4, local copies, waits for them, and re-layouts  3.76 us
    mul x1, other arithmetic, on_device(): totals * scale  1.18 us

profile of v1, /device:TPU:13, one launch (start us, length us, event | category | flops | bytes accessed | tf_op | source)
XLA Modules:
  0.0 42.4 jit_solution(14957345474134803244)
XLA Ops:
  2.6 0.0 copy-start
  2.6 6.6 %tomography.1 = (f32[8,32,128]{2,1,0:T(8,128)}, f32[8,16,512]{2,1,0:T(8,128)}, f32[8,128]{1,0:T(8,128)}) custom-call(s32[64]{0:T(128)} %rows_ref.1, s32[64]{0:T(128)} %cols_ref.1, f32[1]{0:T(128)S(6)} %copy.21.rate_ref, f32[8,16,512]{2,1,0:T(8,128)} %bitcast.12, f32[8,32,128]{2,1,0:T(8,128)} %bitcast.18, f32[8,32,128]{2,1,0:T(8,128)} %bitcast.19, ...), custom_call_target="tpu_custom_call" | custom-call | tf_op jit(solution)/shard_map/tomography/pallas_call | solution.py:388
  9.2 28.2 %variation.1 = (f32[8,16,512]{2,1,0:T(8,128)}, f32[3,8,16,512]{3,2,1,0:T(8,128)}, f32[2]{0:T(128)}) custom-call(f32[1]{0:T(128)S(6)} %copy.21.rate_ref, f32[1]{0:T(128)S(6)} %copy.22.primal_ref, f32[1]{0:T(128)S(6)} %copy.23.reg_ref, f32[8,16,512]{2,1,0:T(8,128)} %bitcast.16, f32[8,16,512]{2,1,0:T(8,128)} %bitcast.13, f32[3,8,16,512]{3,2,1,0:T(8,128)} %bitcast.14, ...), custom_call_target="tpu_custom_call" | custom-call | tf_op jit(solution)/shard_map/variation/pallas_call | solution.py:411
  37.4 0.0 copy-done
  37.4 1.2 %mul.3 = f32[2]{0:T(128)} multiply(f32[2]{0:T(128)} %get-tuple-element.15, f32[2]{0:T(128)S(1)} %copy-done) | non-fusion elementwise | flops 2 | bytes 24 | tf_op jit(solution)/shard_map/mul | solution.py:444
  38.6 1.7 %copy.24 = f32[8,1,16,512]{3,2,1,0:T(8,128)} copy(f32[8,1,16,512]{3,2,1,0:T(8,128)} %bitcast.17) | data formatting | bytes 524288
  40.3 2.1 %copy.25 = f32[3,8,1,16,512]{4,3,2,1,0:T(8,128)} copy(f32[3,8,1,16,512]{4,3,2,1,0:T(8,128)} %bitcast.15) | data formatting | bytes 1572864
Async XLA Ops:
  2.6 34.9 %copy-start = (f32[2]{0:T(128)S(1)}, f32[2]{0:T(128)}, u32[]{:S(2)}) copy-start(f32[2]{0:T(128)} %constant.2.clone) | copy-start | bytes 28

commit v2 on v1

--- a/solution.py
+++ b/solution.py
@@ -31,72 +31,67 @@
         lax.fori_loop(start, stop, step, 0)
 
 
-def tomography(
-    rows_ref, cols_ref, rate_ref, ext_ref, dual_ref, meas_ref, proj_ref,
-    data_ref, back_ref, misfit_ref, image, sino, low, back,
-):
+def chosen(picks, count):
+    spots = lax.broadcasted_iota(jnp.int32, (count, picks.shape[1]), 0)
+    return jnp.where(spots == picks, 1.0, 0.0)
+
+
+def project(picks_ref, source, proj, products, contract):
+    tiles = proj.shape[0]
+    together = math.gcd(tiles, 8)
+
+    def step(turn, carry):
+        base = turn * together
+        for u in range(together):
+            products[base + u] = lax.dot_general(
+                source[picks_ref[base + u]].astype(jnp.bfloat16), proj[base + u],
+                (((1,), (contract,)), ((), ())),
+                preferred_element_type=jnp.float32,
+            )
+        return carry
+
+    lax.fori_loop(0, tiles // together, step, 0)
+
+
+def gathered_sum(selector, products, c):
+    return jnp.dot(selector, products[:, c, :], precision=lax.Precision.HIGHEST,
+                   preferred_element_type=jnp.float32)
+
+
+def forward_part(rate, cols_ref, row_picks, ext_ref, dual_ref, meas_ref, proj,
+                 data_ref, image, low, products):
     channels, row_count, col_count = ext_ref.shape
     per_row = col_count // LANES
-    ray_blocks = sino.shape[0]
-    tiles = proj_ref.shape[0]
-    together = math.gcd(tiles, 8)
-    rate = rate_ref[0]
     for row in range(row_count):
         line = ext_ref[:, row, :].astype(jnp.bfloat16).astype(jnp.float32)
         for q in range(per_row):
             image[row * per_row + q] = line[:, q * LANES : (q + 1) * LANES]
-    sino[...] = jnp.zeros_like(sino)
-    back[...] = jnp.zeros_like(back)
-
-    def forward(step, carry):
-        base = step * together
-        made = []
-        for u in range(together):
-            picked = image[cols_ref[base + u]].astype(jnp.bfloat16)
-            made.append(
-                lax.dot_general(
-                    picked, proj_ref[base + u], (((1,), (1,)), ((), ())),
-                    preferred_element_type=jnp.float32,
-                )
-            )
-        for u in range(together):
-            spot = rows_ref[base + u]
-            sino[spot] = sino[spot] + made[u]
-        return carry
-
-    lax.fori_loop(0, tiles // together, forward, 0)
-
-    inverse = 1.0 / (1.0 + jnp.full((channels, LANES), rate, jnp.float32))
-    misfit = jnp.zeros((channels, LANES), jnp.float32)
-    for r in range(ray_blocks):
-        residual = sino[r] - meas_ref[:, r, :]
-        fresh = (dual_ref[:, r, :] + rate * residual) * inverse
+    project(cols_ref, image, proj, products, 1)
+    ray_blocks = low.shape[0]
+    selector = chosen(row_picks[...], ray_blocks)
+    inverse = 1.0 / (1.0 + jnp.full((ray_blocks, LANES), rate, jnp.float32))
+    misfit = jnp.zeros((ray_blocks, LANES), jnp.float32)
+    for c in range(channels):
+        residual = gathered_sum(selector, products, c) - meas_ref[c]
+        fresh = (dual_ref[c] + rate * residual) * inverse
         misfit = misfit + residual * residual
-        data_ref[:, r, :] = fresh
-        low[r] = fresh
-    misfit_ref[...] = misfit
-
-    def backward(step, carry):
-        base = step * together
-        made = []
-        for u in range(together):
-            picked = low[rows_ref[base + u]].astype(jnp.bfloat16)
-            made.append(
-                lax.dot_general(
-                    picked, proj_ref[base + u], (((1,), (0,)), ((), ())),
-                    preferred_element_type=jnp.float32,
-                )
-            )
-        for u in range(together):
-            spot = cols_ref[base + u]
-            back[spot] = back[spot] + made[u]
-        return carry
-
-    lax.fori_loop(0, tiles // together, backward, 0)
-    for row in range(row_count):
-        back_ref[:, row, :] = jnp.concatenate(
-            [back[row * per_row + q] for q in range(per_row)], axis=1
-        )
+        data_ref[c] = fresh
+        low[:, c, :] = fresh
+    tile = misfit[:SUBS]
+    for r in range(1, ray_blocks // SUBS):
+        tile = tile + misfit[r * SUBS : (r + 1) * SUBS]
+    return tile
+
+
+def backward_part(rows_ref, col_picks, proj, low, products, blocked, back):
+    channels, row_count, col_count = back.shape
+    per_row = col_count // LANES
+    project(rows_ref, low, proj, products, 0)
+    selector = chosen(col_picks[...], row_count * per_row)
+    for c in range(channels):
+        blocked[c] = gathered_sum(selector, products, c)
+        for q in range(per_row):
+            back[c, :, q * LANES : (q + 1) * LANES] = blocked[c, pl.ds(q, row_count, stride=per_row), :]
 
 
 def jacobi_sweep(_, state):
@@ -146,8 +141,10 @@
 
 def variation(
     n, slabs, owners, total_channels,
-    rate_ref, primal_ref, reg_ref, vol_ref, ext_ref, grad_ref, misfit_ref, back_ref,
-    upd_ref, out_ref, totals_ref,
+    rate_ref, primal_ref, reg_ref, rows_ref, cols_ref, row_picks, col_picks,
+    ext_ref, vol_hbm, grad_hbm, dual_hbm, meas_hbm, proj_hbm,
+    upd_ref, out_ref, data_ref, totals_ref,
+    vol_ref, grad_ref, dual_ref, meas_ref, proj, image, low, products, blocked, back_ref, load_sem,
     foll, prior, cand, level, part, gathered, fac, fac_image, sums,
     foll_send, foll_recv, prior_send, prior_recv,
     part_send, part_recv, fac_send, fac_recv, sum_send, sum_recv,
@@ -164,6 +161,14 @@
     primal = primal_ref[0]
     radius = reg_ref[0] * math.sqrt(total_channels)
 
+    loads = [
+        pltpu.make_async_copy(src, dst, load_sem.at[i])
+        for i, (src, dst) in enumerate((
+            (proj_hbm, proj), (dual_hbm, dual_ref), (meas_hbm, meas_ref),
+            (grad_hbm, grad_ref), (vol_hbm, vol_ref)))
+    ]
+    for load in loads:
+        load.start()
     barrier = pltpu.get_barrier_semaphore()
 
     def greet_chan(i):
@@ -229,6 +234,11 @@
         return g2 + c2 * c2, g4 + cand[0, c] * c2, g5 + cand[1, c] * c2
 
     nothing = jnp.zeros((row_count, col_count), jnp.float32)
+    for load in loads[:3]:
+        load.wait()
+    misfit = forward_part(rate, cols_ref, row_picks, ext_ref, dual_ref, meas_ref, proj,
+                          data_ref, image, low, products)
+    loads[3].wait()
     g0, g1, g3 = lax.fori_loop(0, channels, flat, (nothing,) * 3)
     g2, g4, g5 = lax.fori_loop(0, channels, deep, (nothing,) * 3)
     grams = (g0, g1, g2, g3, g4, g5)
@@ -241,7 +251,7 @@
         rows, cols = place(b)
         for e in range(6):
             part[b, e] = grams[e][rows, cols]
-        part[b, 6] = misfit_ref[...]
+        part[b, 6] = misfit
 
     def if_owner(index, body):
         if owners == n:
@@ -283,6 +293,7 @@
             fac[base + o, 7] = total[o, 6]
         each(1, n, lambda i: fac_copy(i).start())
 
+    backward_part(rows_ref, col_picks, proj, low, products, blocked, back_ref)
     if_owner(me, diagonalize)
     each(1, n, lambda i: if_owner(lax.rem(me - i + n, n), lambda: fac_copy(i).wait_recv()))
 
@@ -323,6 +334,8 @@
     lax.fori_loop(0, channels, depth, 0)
     each(1, slabs, lambda i: sum_copy(i).start())
     kept = jnp.where(last, 0.0, 1.0)
+
+    loads[4].wait()
 
     def plane(c, carry):
         n0 = turned(c, 0)
@@ -385,39 +398,34 @@
     extrapolated = extrapolated.reshape(image_shape)
     dual_grad = dual_grad.reshape((3,) + image_shape)
     ray_shape = (channels, rays // LANES, LANES)
-    data_new, back, misfit = pl.pallas_call(
-        tomography,
-        out_shape=(
-            jax.ShapeDtypeStruct(ray_shape, f32),
-            jax.ShapeDtypeStruct(image_shape, f32),
-            jax.ShapeDtypeStruct((channels, LANES), f32),
-        ),
-        in_specs=[smem] * 3 + [vmem] * 4,
-        out_specs=(vmem,) * 3,
-        scratch_shapes=[
-            pltpu.VMEM((pixels // LANES, channels, LANES), f32),
-            pltpu.VMEM((rays // LANES, channels, LANES), f32),
-            pltpu.VMEM((rays // LANES, channels, LANES), f32),
-            pltpu.VMEM((pixels // LANES, channels, LANES), f32),
-        ],
-        name="tomography",
-    )(tile_rows, tile_cols, dual_step, extrapolated, dual_data.reshape(ray_shape),
-      measured.reshape(ray_shape), projector)
-
     blocks = pixels // (SUBS * LANES)
     owners = math.gcd(n, blocks)
     own = blocks // owners
     dma = pltpu.SemaphoreType.DMA
-    updated, grad_new, totals = pl.pallas_call(
+    hbm = pl.BlockSpec(memory_space=pl.ANY)
+    tiles = projector.shape[0]
+    updated, grad_new, data_new, totals = pl.pallas_call(
         functools.partial(variation, n, slabs, owners, channels * n),
         out_shape=(
             jax.ShapeDtypeStruct(image_shape, f32),
             jax.ShapeDtypeStruct((3,) + image_shape, f32),
+            jax.ShapeDtypeStruct(ray_shape, f32),
             jax.ShapeDtypeStruct((2,), f32),
         ),
-        in_specs=[smem] * 3 + [vmem] * 5,
-        out_specs=(vmem, vmem, smem),
+        in_specs=[smem] * 5 + [vmem] * 3 + [hbm] * 5,
+        out_specs=(vmem, vmem, vmem, smem),
         scratch_shapes=[
+            pltpu.VMEM(image_shape, f32),
+            pltpu.VMEM((3,) + image_shape, f32),
+            pltpu.VMEM(ray_shape, f32),
+            pltpu.VMEM(ray_shape, f32),
+            pltpu.VMEM(projector.shape, projector.dtype),
+            pltpu.VMEM((pixels // LANES, channels, LANES), f32),
+            pltpu.VMEM((rays // LANES, channels, LANES), f32),
+            pltpu.VMEM((tiles, channels, LANES), f32),
+            pltpu.VMEM((channels, pixels // LANES, LANES), f32),
+            pltpu.VMEM(image_shape, f32),
+            pltpu.SemaphoreType.DMA((5,)),
             pltpu.VMEM(image_shape, f32),
             pltpu.VMEM(image_shape, f32),
             pltpu.VMEM((3,) + image_shape, f32),
@@ -433,7 +441,9 @@
         ],
         compiler_params=pltpu.CompilerParams(collective_id=0, has_side_effects=True),
         name="variation",
-    )(dual_step, primal_step, reg_weight, volume_now, extrapolated, dual_grad, misfit, back)
+    )(dual_step, primal_step, reg_weight, tile_rows, tile_cols,
+      tile_rows.reshape(1, tiles), tile_cols.reshape(1, tiles), extrapolated, volume_now,
+      dual_grad, dual_data.reshape(ray_shape), measured.reshape(ray_shape), projector)
     scale = jnp.asarray([1.0 / (channels * n * slabs * slices * rays),
                          1.0 / (slabs * slices * pixels)], f32)
     full = (channels, slices, row_count, col_count)

time: 43 us -> 37.4 us (0.87)
  Pallas kernels: 34.8 us -> 28.9 us
  local copies, waits for them, and re-layouts: 3.76 us -> 4.42 us
    pallas_call x1 -> x0, Pallas kernels: 6.62 us -> none  [on_device(): pl.pallas_call(tomography, out_shape=(jax.ShapeDtypeStruct(ray_shape, f32...]
    unnamed x4 -> x7, local copies, waits for them, and re-layouts: 3.76 us -> 4.42 us
    pallas_call x1, Pallas kernels: 28.2 us -> 28.9 us  [on_device(): pl.pallas_call(functools.partial(variation, n, slabs, owners, channels *...]
where the time goes in v2:
time: 37.4 us; the launch traced here: 37.1 us
  Pallas kernels  28.9 us (77%)
  local copies, waits for them, and re-layouts  4.42 us (12%)
  between operations  2.62 us (7%)
  other arithmetic  1.17 us (3%)
    pallas_call x1, Pallas kernels, on_device(): pl.pallas_call(functools.partial(variation, n, slabs, owners, channels *...  28.9 us
    unnamed x7, local copies, waits for them, and re-layouts  4.42 us
    mul x1, other arithmetic, on_device(): totals * scale  1.17 us

profile of v2, /device:TPU:13, one launch (start us, length us, event | category | flops | bytes accessed | tf_op | source)
XLA Modules:
  0.0 37.1 jit_solution(13781607234272528032)
XLA Ops:
  0.6 0.0 copy-start.1
  2.6 28.9 %variation.1 = (f32[8,16,512]{2,1,0:T(8,128)}, f32[3,8,16,512]{3,2,1,0:T(8,128)}, f32[8,32,128]{2,1,0:T(8,128)}, f32[2]{0:T(128)}) custom-call(f32[1]{0:T(128)S(6)} %copy.22.rate_ref, f32[1]{0:T(128)S(6)} %copy.23.primal_ref, f32[1]{0:T(128)S(6)} %copy.24.reg_ref, s32[64]{0:T(128)} %rows_ref.1, s32[64]{0:T(128)} %cols_ref.1, s32[1,64]{1,0:T(1,128)} %bitcast.22, ...), custom_call_target="tpu_custom_call" | custom-call | tf_op jit(solution)/shard_map/variation/pallas_call | solution.py:407
  31.5 0.0 copy-start
  31.5 0.0 copy-done.1
  31.5 1.2 %mul.3 = f32[2]{0:T(128)} multiply(f32[2]{0:T(128)} %get-tuple-element.11, f32[2]{0:T(128)S(1)} %copy-done.1) | non-fusion elementwise | flops 2 | bytes 24 | tf_op jit(solution)/shard_map/mul | solution.py:454
  32.7 1.7 %copy.25 = f32[8,1,16,512]{3,2,1,0:T(8,128)} copy(f32[8,1,16,512]{3,2,1,0:T(8,128)} %bitcast.16) | data formatting | bytes 524288
  34.3 2.1 %copy.26 = f32[3,8,1,16,512]{4,3,2,1,0:T(8,128)} copy(f32[3,8,1,16,512]{4,3,2,1,0:T(8,128)} %bitcast.14) | data formatting | bytes 1572864
  36.4 0.0 copy-done
  36.4 0.7 %copy.27 = f32[8,1,4096]{2,1,0:T(1,128)} copy(f32[8,1,4096]{2,1,0:T(1,128)S(1)} %bitcast.21) | data formatting | bytes 262144
Async XLA Ops:
  0.6 30.9 %copy-start.1 = (f32[2]{0:T(128)S(1)}, f32[2]{0:T(128)}, u32[]{:S(2)}) copy-start(f32[2]{0:T(128)} %constant.2.clone) | copy-start | bytes 28
  31.5 5.0 %copy-start = (f32[8,32,128]{2,1,0:T(8,128)S(1)}, f32[8,32,128]{2,1,0:T(8,128)}, u32[]{:S(2)}) copy-start(f32[8,32,128]{2,1,0:T(8,128)} %get-tuple-element.10) | copy-start | bytes 393220

commit v3 on v2

--- a/solution.py
+++ b/solution.py
@@ -407,9 +407,9 @@
     updated, grad_new, data_new, totals = pl.pallas_call(
         functools.partial(variation, n, slabs, owners, channels * n),
         out_shape=(
-            jax.ShapeDtypeStruct(image_shape, f32),
-            jax.ShapeDtypeStruct((3,) + image_shape, f32),
-            jax.ShapeDtypeStruct(ray_shape, f32),
+            pltpu.VMEM(image_shape, f32),
+            pltpu.VMEM((3,) + image_shape, f32),
+            pltpu.VMEM(ray_shape, f32),
             jax.ShapeDtypeStruct((2,), f32),
         ),
         in_specs=[smem] * 5 + [vmem] * 3 + [hbm] * 5,

time: 37.4 us -> 33.9 us (0.906)
  local copies, waits for them, and re-layouts: 4.42 us -> 2.25 us
  other arithmetic: 1.17 us -> 0.51 us
  Pallas kernels: 28.9 us -> 28.4 us
    unnamed x7, local copies, waits for them, and re-layouts: 4.42 us -> 2.25 us
    mul x1, other arithmetic: 1.17 us -> 0.51 us  [on_device(): totals * scale]
    pallas_call x1, Pallas kernels: 28.9 us -> 28.4 us  [on_device(): pl.pallas_call(functools.partial(variation, n, slabs, owners, channels *...]
where the time goes in v3:
time: 33.9 us; the launch traced here: 33.8 us
  Pallas kernels  28.4 us (84%)
  between operations  2.6 us (8%)
  local copies, waits for them, and re-layouts  2.25 us (7%)
  other arithmetic  0.51 us (2%)
    pallas_call x1, Pallas kernels, on_device(): pl.pallas_call(functools.partial(variation, n, slabs, owners, channels *...  28.4 us
    unnamed x7, local copies, waits for them, and re-layouts  2.25 us

profile of v3, /device:TPU:13, one launch (start us, length us, event | category | flops | bytes accessed | tf_op | source)
XLA Modules:
  0.0 33.8 jit_solution(10615721606365664791)
XLA Ops:
  2.6 0.0 copy-start.1
  2.6 28.4 %variation.1 = (f32[8,16,512]{2,1,0:T(8,128)S(1)}, f32[3,8,16,512]{3,2,1,0:T(8,128)S(1)}, f32[8,32,128]{2,1,0:T(8,128)S(1)}, f32[2]{0:T(128)}) custom-call(f32[1]{0:T(128)S(6)} %copy.25.rate_ref, f32[1]{0:T(128)S(6)} %copy.26.primal_ref, f32[1]{0:T(128)S(6)} %copy.27.reg_ref, s32[64]{0:T(128)} %rows_ref.1, s32[64]{0:T(128)} %cols_ref.1, s32[1,64]{1,0:T(1,128)} %bitcast.22, ...), custom_call_target="tpu_custom_call" | custom-call | tf_op jit(solution)/shard_map/variation/pallas_call | solution.py:407
  31.0 0.0 copy-start
  31.0 0.7 %copy.22 = f32[8,1,16,512]{3,2,1,0:T(8,128)} copy(f32[8,1,16,512]{3,2,1,0:T(8,128)S(1)} %bitcast.15) | data formatting | bytes 524288
  31.7 0.9 %copy.23 = f32[3,8,1,16,512]{4,3,2,1,0:T(8,128)} copy(f32[3,8,1,16,512]{4,3,2,1,0:T(8,128)S(1)} %bitcast.14) | data formatting | bytes 1572864
  32.6 0.0 copy-done.1
  32.6 0.0 copy-done
  32.6 0.5 %mul.3 = f32[2]{0:T(128)} multiply(f32[2]{0:T(128)S(1)} %copy-done, f32[2]{0:T(128)S(1)} %copy-done.1) | non-fusion elementwise | flops 2 | bytes 24 | tf_op jit(solution)/shard_map/mul | solution.py:454
  33.1 0.7 %copy.24 = f32[8,1,4096]{2,1,0:T(1,128)} copy(f32[8,1,4096]{2,1,0:T(1,128)S(1)} %bitcast.16) | data formatting | bytes 262144
Async XLA Ops:
  2.6 30.0 %copy-start.1 = (f32[2]{0:T(128)S(1)}, f32[2]{0:T(128)}, u32[]{:S(2)}) copy-start(f32[2]{0:T(128)} %constant.2.clone) | copy-start | bytes 28
  31.0 1.6 %copy-start = (f32[2]{0:T(128)S(1)}, f32[2]{0:T(128)}, u32[]{:S(2)}) copy-start(f32[2]{0:T(128)} %get-tuple-element.11) | copy-start | bytes 28
